TPU v7x, 8 devices: a whole 2x2x1 slice. The times are simulated.
8 devices in a mesh: dp: 2 (over y, z), sp: 4 (over x, core).
Axes of the slice: x: 2, y: 2, z: 1, core: 2. Of those that a mesh axis runs over, the one named last changes fastest.
Arguments:
- q: bfloat16 [64, 32, 256], P('dp'), parts along dimension 0
- k: bfloat16 [64, 8192, 1, 256], P('dp', 'sp'), parts along dimension 0
- v: bfloat16 [64, 8192, 1, 256], P('dp', 'sp'), parts along dimension 0
Outputs:
- q: bfloat16 [64, 32, 256], P('dp'), parts along dimension 0
There are 2 independent parts. A program takes and returns all parts, laid end to end along the dimension named above; each array names one.
All inputs are finite; a program needn't handle non-finite values.
Results may differ from a plain program's by a relative error of at most 0.012.
Values are sent between devices in bfloat16 or wider.
A program may use at most 2 GiB of HBM per device.

v0:
```python
import jax
import jax.numpy as jnp
from jax import lax
from jax.sharding import PartitionSpec as P


def einsum(form, a, b):
    return jnp.einsum(form, a.astype(jnp.float32), b.astype(jnp.float32))


def part_of(q, k, v):
    grouped = q.reshape(q.shape[0], k.shape[2], -1, q.shape[2])
    scores = einsum("bgsd,bugd->bgsu", grouped, k) * q.shape[2] ** -0.5
    high = jnp.max(scores, -1, keepdims=True)
    weights = jnp.exp(scores - high)
    seen = einsum("bgsu,bugd->bgsd", weights.astype(jnp.bfloat16), v)
    return jnp.concatenate([seen, jnp.sum(weights, -1, keepdims=True), high], -1)


def together(parts):
    seen, total, high = parts[..., :-2], parts[..., -2:-1], parts[..., -1:]
    scale = jnp.exp(high - jnp.max(high, 0))
    return (jnp.sum(seen * scale, 0) / jnp.sum(total * scale, 0)).astype(jnp.bfloat16)


def solution(mesh):
    def step(q, k, v):
        return together(lax.all_gather(part_of(q, k, v), "sp")).reshape(q.shape)

    return jax.shard_map(
        step,
        mesh=mesh,
        in_specs=(P("dp", None, None), P("dp", "sp", None, None), P("dp", "sp", None, None)),
        out_specs=P("dp", None, None),
        check_vma=False,
    )
```

profile of v0, /device:TPU:0, one launch (start us, length us, event | category | flops | bytes accessed | tf_op | source)
XLA Modules:
  0.0 133.3 jit_solution(9702489174152530521)
XLA Ops:
  6.5 0.0 copy-start
  6.5 0.0 all-gather.3.cloned.1.call-start
  6.5 1.0 copy-done
  7.6 19.0 %multiply_reduce_fusion = (f32[32,32]{1,0:T(8,128)S(1)}, f32[32,32,2048]{2,1,0:T(8,128)}) fusion(bf16[32,32,256]{2,1,0:T(8,128)(2,1)S(1)} %copy-done, bf16[32,2048,1,256]{3,1,2,0:T(8,128)(2,1)} %param.4), kind=kOutput, calls=%fused_computation.7 | convolution fusion | flops 1077935104 | bytes 42471424 | tf_op jit(solution)/shard_map/bgsd,bugd->bgsu/dot_general | solution.py:8
  26.6 4.3 %fusion.5 = f32[32,32]{1,0:T(8,128)S(1)} fusion(f32[32,32,2048]{2,1,0:T(8,128)} %get-tuple-element.8, f32[32,32]{1,0:T(8,128)S(1)} %get-tuple-element.7), kind=kLoop, calls=%fused_computation.8 | loop fusion | flops 6290432 | bytes 8396800 | tf_op jit(solution)/shard_map/reduce_sum | solution.py:17
  30.9 15.8 %fusion.10 = f32[32,1,32,256]{3,2,0,1:T(8,128)S(1)} fusion(bf16[32,2048,1,256]{3,1,2,0:T(8,128)(2,1)} %param.5, f32[32,32,2048]{2,1,0:T(8,128)} %get-tuple-element.8, f32[32,32]{1,0:T(8,128)S(1)} %get-tuple-element.7), kind=kOutput, calls=%fused_computation.13 | convolution fusion | flops 1080033280 | bytes 42995712 | tf_op jit(solution)/shard_map/bgsu,bugd->bgsd/dot_general | solution.py:8
  46.7 0.3 copy.17
  47.0 0.3 copy.18
  47.2 1.4 %maximum_bitcast_fusion = f32[32,1,32,258]{3,2,1,0:T(8,128)} fusion(f32[32,1,32,1]{3,2,0,1:T(8,128)S(1)} %copy.18, f32[32,1,32,1]{3,2,0,1:T(8,128)S(1)} %copy.17, f32[32,1,32,256]{3,2,0,1:T(8,128)S(1)} %fusion.10), kind=kLoop, calls=%fused_computation.12 | loop fusion | flops 528384 | bytes 2113536 | tf_op jit(solution)/shard_map/concatenate | solution.py:17
  48.7 0.0 all-gather.3.cloned.1.call-update
  48.7 46.6 %all-gather.3.cloned.1.call-done = f32[128,1,32,258]{3,2,1,0:T(8,128)} async-done(((f32[32,1,32,258]{3,2,1,0:T(8,128)}), f32[128,1,32,258]{3,2,1,0:T(8,128)}) %all-gather.3.cloned.1.call-update) | async-done | bytes 4227088 | tf_op jit(solution)/shard_map/all_gather | solution.py:28
  95.3 14.0 %copy.20 = f32[128,1,32,258]{2,0,3,1:T(8,128)} copy(f32[128,1,32,258]{3,2,1,0:T(8,128)} %all-gather.3.cloned.1.call-done) | data formatting | bytes 8454144 | tf_op jit(solution)/shard_map/all_gather | solution.py:28
  109.3 0.9 slice_reduce_fusion
  110.1 0.9 fusion.15
  111.0 0.0 copy-start.1
  111.0 10.9 %fusion.4 = f32[32,32,256]{1,0,2:T(8,128)} fusion(f32[4,32,1,32,258]{3,1,0,4,2:T(8,128)} %bitcast.22, f32[4,32,32]{2,1,0:T(8,128)S(1)} %get-tuple-element.6), kind=kLoop, calls=%fused_computation.5 | loop fusion | flops 1835008 | bytes 5259264 | tf_op jit(solution)/shard_map/reduce_sum | solution.py:23
  122.0 3.5 %copy.21 = f32[32,32,256]{2,1,0:T(8,128)S(1)} copy(f32[32,32,256]{1,0,2:T(8,128)} %fusion.4) | data formatting | bytes 2097152 | tf_op jit(solution)/shard_map/reduce_sum | solution.py:23
  125.5 1.0 divide_convert_fusion
  126.5 0.0 copy-done.1
Async XLA Ops:
  6.5 1.0 copy-start
  6.5 88.8 %all-gather.3.cloned.1.call-start = ((), (), s32[]{:S(2)}) async-start(), calls=%async_computation | async-start | bytes 7864320 | tf_op jit(solution)/shard_map/all_gather | solution.py:28
  111.0 15.5 %copy-start.1 = (bf16[32,32,256]{2,1,0:T(8,128)(2,1)S(1)}, bf16[32,32,256]{2,1,0:T(8,128)(2,1)}, u32[]{:S(2)}) copy-start(bf16[32,32,256]{2,1,0:T(8,128)(2,1)} %param.3) | copy-start | bytes 1572868
Sparse Core Ops, SparseCore 0:
  48.8 46.4 all-gather.2
where the time goes:
time: 134 us; the launch traced here: 133 us
  waiting for transfers between devices  46.6 us (35%)
  matrix products  34.8 us (26%)
  other arithmetic  19.4 us (14%)
  local copies, waits for them, and re-layouts  19.1 us (14%)
  between operations  13.4 us (10%)
    all_gather x1, waiting for transfers between devices, step(): return together(lax.all_gather(part_of(q, k, v), 'sp')).reshape(q.shape)  46.6 us
    dot_general x2, matrix products, einsum(): return jnp.einsum(form, a.astype(jnp.float32), b.astype(jnp.float32))  34.8 us
    all_gather x1, local copies, waits for them, and re-layouts, step(): return together(lax.all_gather(part_of(q, k, v), 'sp')).reshape(q.shape)  14 us
    reduce_sum x1, other arithmetic, together(): jnp.sum(seen * scale, 0) / jnp.sum(total * scale, 0)  10.9 us
    reduce_sum x1, other arithmetic, part_of(): jnp.sum(weights, -1, keepdims=True)  4.27 us
    reduce_sum x1, local copies, waits for them, and re-layouts, together(): jnp.sum(seen * scale, 0) / jnp.sum(total * scale, 0)  3.51 us
  transfers between devices with their start and end apart: 1, of which 1 were waited for; matrix products, arithmetic and copies ran while one was open for 0% of the time, Pallas kernels for 0%

commit v1 on v0

v1 whole, which is shorter than its diff:
```python
import jax
import jax.numpy as jnp
from jax import lax
from jax.experimental import pallas as pl
from jax.experimental.pallas import tpu as pltpu
from jax.sharding import PartitionSpec as P

MESH = pl.DeviceIdType.MESH
GROUP = 4
SLOTS = 16
LEAD = 2
LOG2E = 1.4426950408889634
EXPLICIT = False


def kernel(mesh, q_hbm, k_hbm, v_hbm, o_ref, *scratch):
    def body(*accs):
        attend(q_hbm, k_hbm, v_hbm, o_ref, accs, *scratch)

    if not EXPLICIT:
        return body()
    with jax.sharding.use_abstract_mesh(mesh.abstract_mesh):
        acc = [pltpu.ACC(m)((32, 256), jnp.float32) for m in (0, 1)]
        pl.run_scoped(body, *[acc[0]] * 6, *[acc[1]] * 6)


def attend(q_hbm, k_hbm, v_hbm, o_ref, accs, q_ref, kbuf, vbuf, scores, weights, mine, theirs, part, pair, from_chip, from_core,
           q_sem, k_sem, v_sem, mine_sem, theirs_sem, part_sem, chip_sem, pair_sem, core_sem):
    count, heads, head = q_hbm.shape
    tokens = k_hbm.shape[1]
    tiles = tokens // 256
    groups = count // GROUP
    factor = head**-0.5 * LOG2E

    dp, sp = lax.axis_index("dp"), lax.axis_index("sp")
    core = sp + 1 - 2 * lax.rem(sp, 2)
    chip = lax.rem(sp + 2, 4)
    across = lax.rem(core + 2, 4)
    peers = (core, chip, across)

    def keys(s):
        return pltpu.make_async_copy(k_hbm.at[s], kbuf.at[s % SLOTS], k_sem.at[s % SLOTS])

    def values(s):
        return pltpu.make_async_copy(v_hbm.at[s], vbuf.at[s % SLOTS], v_sem.at[s % SLOTS])

    def remote(src, dst, send, recv, peer):
        return pltpu.make_async_remote_copy(src, dst, send, recv, device_id=(dp, peer), device_id_type=MESH)

    def stats(g, n):
        return remote(mine.at[g], theirs.at[g, n], mine_sem.at[g, n], theirs_sem.at[g, n], peers[n])

    def to_chip(lo, n):
        return remote(part.at[pl.ds(lo, n)], from_chip.at[pl.ds(lo, n)], part_sem.at[lo], chip_sem.at[lo], chip)

    def to_core(lo, n):
        return remote(pair.at[pl.ds(lo, n)], from_core.at[pl.ds(lo, n)], pair_sem.at[lo], core_sem.at[lo], core)

    def score(s, j):
        q, k = q_ref[s], kbuf.at[s % SLOTS]
        if not EXPLICIT:
            scores[j] = lax.dot_general(q, k[...], (((1,), (1,)), ((), ())), preferred_element_type=jnp.float32)
            return
        for t in range(tiles):
            m, u = t % 2, t // 2
            pltpu.matmul_push_rhs(k[t * 256 : (t + 1) * 256, :], u % 2, m, transpose=True)
            pltpu.matmul_acc_lhs(accs[6 * m + u], q, load_staged_rhs=u % 2)
        for t in range(tiles):
            scores[j, :, t * 256 : (t + 1) * 256] = pltpu.matmul_pop(accs[6 * (t % 2) + t // 2])

    def softmax(s, j):
        x = scores[j]
        high = jnp.max(x, 1, keepdims=True)
        w = jnp.exp2((x - high) * factor)
        weights[s % (LEAD * GROUP)] = w.astype(jnp.bfloat16)
        return high, jnp.sum(w, 1, keepdims=True)

    def gather(s, j):
        w, v = weights.at[s % (LEAD * GROUP)], vbuf.at[s % SLOTS]
        if not EXPLICIT:
            return jnp.dot(w[...], v[...], preferred_element_type=jnp.float32)
        for t in range(tiles):
            m, u = t % 2, t // 2
            pltpu.matmul_push_rhs(v[t * 256 : (t + 1) * 256, :], u % 2, m)
            pltpu.matmul_acc_lhs(accs[6 * m + 4 + j % 2], w[:, t * 256 : (t + 1) * 256], load_staged_rhs=u % 2)
        return pltpu.matmul_pop(accs[4 + j % 2]) + pltpu.matmul_pop(accs[10 + j % 2])

    def keep_stats(g, pairs):
        lane = lax.broadcasted_iota(jnp.int32, (heads, 128), 1)
        x = jnp.zeros((heads, 128), jnp.float32)
        for j, (high, total) in enumerate(pairs):
            x = jnp.where(lane == j, high, x)
            x = jnp.where(lane == GROUP + j, total, x)
        mine[g, :, :heads] = x.T[: 2 * GROUP, :]

    def shares(g):
        rows = [mine[g]] + [theirs[g, n] for n in range(3)]
        highs, totals = [r[:GROUP] for r in rows], [r[GROUP:] for r in rows]
        top = jnp.maximum(jnp.maximum(highs[0], highs[1]), jnp.maximum(highs[2], highs[3]))
        scale = [jnp.exp2((h - top) * factor) for h in highs]
        parts = [t * s for t, s in zip(totals, scale)]
        whole = (parts[0] + parts[1]) + (parts[2] + parts[3])
        share = scale[0] / whole
        return jnp.concatenate([share, jnp.zeros_like(share)], 0).T

    def add_chip(lo, n):
        a = part[lo : lo + n].astype(jnp.float32) + from_chip[lo : lo + n].astype(jnp.float32)
        pair[lo : lo + n] = a.astype(jnp.bfloat16)

    def add_core(lo, n):
        a = pair[lo : lo + n].astype(jnp.float32) + from_core[lo : lo + n].astype(jnp.float32)
        o_ref[lo : lo + n] = a.astype(jnp.bfloat16)

    pltpu.make_async_copy(q_hbm, q_ref, q_sem.at[0]).start()
    for s in range(LEAD * GROUP):
        keys(s).start()
    for s in range(SLOTS - LEAD * GROUP):
        keys(s + LEAD * GROUP).start()
        values(s).start()
    barrier = pltpu.get_barrier_semaphore()
    for peer in peers:
        pl.semaphore_signal(barrier, inc=1, device_id=(dp, peer), device_id_type=MESH)
    pltpu.make_async_copy(q_hbm, q_ref, q_sem.at[0]).wait()

    for h in range(groups + LEAD):
        g = h - LEAD
        with_keys, with_values = h < groups, g >= 0
        if with_keys and with_values and h < groups - 1:
            for j in range(GROUP):
                keys(GROUP * h + j).wait()
                values(GROUP * g + j).wait()
        if with_values:
            for n in range(3):
                stats(g, n).wait_recv()
            share = shares(g)
            if g >= 2:
                to_chip(GROUP * (g - 2), GROUP).wait_recv()
                add_chip(GROUP * (g - 2), GROUP)
            if g >= 3:
                to_core(GROUP * (g - 3), GROUP).wait_recv()
                add_core(GROUP * (g - 3), GROUP)
        pairs = []
        for j in range(GROUP):
            sk, sv = GROUP * h + j, GROUP * g + j
            alone = not (with_keys and with_values) or h == groups - 1
            if with_keys:
                if alone:
                    keys(sk).wait()
                score(sk, j)
            if with_values:
                if alone:
                    values(sv).wait()
                seen = gather(sv, j)
                part[sv] = (seen * share[:heads, j : j + 1]).astype(jnp.bfloat16)
            if with_keys:
                pairs.append(softmax(sk, j))
        if with_keys:
            keep_stats(h, pairs)
            if h == 0:
                pl.semaphore_wait(barrier, 3)
            for n in range(3):
                stats(h, n).start()
        if with_values:
            to_chip(GROUP * g, GROUP).start()
            if g >= 2:
                to_core(GROUP * (g - 2), GROUP).start()
        for j in range(GROUP):
            if GROUP * h + SLOTS + j < count:
                keys(GROUP * h + SLOTS + j).start()
            if GROUP * (g + 4) + j < count and GROUP * (g + 4) + j >= SLOTS - LEAD * GROUP:
                values(GROUP * (g + 4) + j).start()

    for g in range(groups - 2, groups):
        to_chip(GROUP * g, GROUP).wait_recv()
        add_chip(GROUP * g, GROUP)
        to_core(GROUP * g, GROUP).start()
    for g in range(groups - 3, groups):
        to_core(GROUP * g, GROUP).wait_recv()
        add_core(GROUP * g, GROUP)
    for g in range(groups):
        for n in range(3):
            stats(g, n).wait_send()
        to_chip(GROUP * g, GROUP).wait_send()
        to_core(GROUP * g, GROUP).wait_send()


def solution(mesh):
    def step(q, k, v):
        count, heads, head = q.shape
        tokens = k.shape[1]
        groups = count // GROUP
        whole = (count, heads, head)
        dma = pltpu.SemaphoreType.DMA
        return pl.pallas_call(
            lambda *refs: kernel(mesh, *refs),
            out_shape=jax.ShapeDtypeStruct(whole, jnp.bfloat16),
            in_specs=[pl.BlockSpec(memory_space=pl.ANY)] * 3,
            out_specs=pl.BlockSpec(memory_space=pltpu.VMEM),
            scratch_shapes=[
                pltpu.VMEM(whole, jnp.bfloat16),
                pltpu.VMEM((SLOTS, tokens, head), jnp.bfloat16),
                pltpu.VMEM((SLOTS, tokens, head), jnp.bfloat16),
                pltpu.VMEM((GROUP, heads, tokens), jnp.float32),
                pltpu.VMEM((LEAD * GROUP, heads, tokens), jnp.bfloat16),
                pltpu.VMEM((groups, 2 * GROUP, 128), jnp.float32),
                pltpu.VMEM((groups, 3, 2 * GROUP, 128), jnp.float32),
                *[pltpu.VMEM(whole, jnp.bfloat16)] * 4,
                dma((1,)),
                dma((SLOTS,)),
                dma((SLOTS,)),
                dma((groups, 3)),
                dma((groups, 3)),
                *[dma((count,))] * 4,
            ],
            compiler_params=pltpu.CompilerParams(collective_id=0, has_side_effects=True, vmem_limit_bytes=60 * 2**20),
            name="attend",
        )(q, k.reshape(count, tokens, head), v.reshape(count, tokens, head))

    return jax.shard_map(
        step,
        mesh=mesh,
        in_specs=(P("dp", None, None), P("dp", "sp", None, None), P("dp", "sp", None, None)),
        out_specs=P("dp", None, None),
        check_vma=False,
    )
```

time: 134 us -> 48.4 us (0.36)
  waiting for transfers between devices: 46.6 us -> 0 us
  Pallas kernels: 0 us -> 46.4 us
  matrix products: 34.8 us -> 0 us
  other arithmetic: 19.4 us -> 0 us
  local copies, waits for them, and re-layouts: 19.1 us -> 1.87 us
  between operations: 13.4 us -> 0.01 us
    all_gather x1 -> x0, waiting for transfers between devices: 46.6 us -> none  [step(): return together(lax.all_gather(part_of(q, k, v), 'sp')).reshape(q.shape)]
    pallas_call x0 -> x1, Pallas kernels: none -> 46.4 us  [step(): pl.pallas_call(lambda *refs: kernel(mesh, *refs), out_shape=jax.ShapeDtyp...]
    dot_general x2 -> x0, matrix products: 34.8 us -> none  [einsum(): return jnp.einsum(form, a.astype(jnp.float32), b.astype(jnp.float32))]
    reduce_sum x3 -> x0, other arithmetic: 16.1 us -> none  [the longest x1 10.9 us: together(): jnp.sum(seen * scale, 0) / jnp.sum(total * scale, 0)]
    all_gather x1 -> x0, local copies, waits for them, and re-layouts: 14 us -> none  [step(): return together(lax.all_gather(part_of(q, k, v), 'sp')).reshape(q.shape)]
    reduce_sum x1 -> x0, local copies, waits for them, and re-layouts: 3.51 us -> none  [together(): jnp.sum(seen * scale, 0) / jnp.sum(total * scale, 0)]
    concatenate x1 -> x0, other arithmetic: 1.43 us -> none  [part_of(): jnp.concatenate([seen, jnp.sum(weights, -1, keepdims=True), high], -1)]
  transfers between devices with their start and end apart: 1 -> 0, of which waited for: 1 -> 0; matrix products, arithmetic and copies ran while one was open for 0% -> 0% of each run, Pallas kernels for 0% -> 0%
where the time goes in v1:
time: 48.4 us; the launch traced here: 48.3 us
  Pallas kernels  46.4 us (96%)
  local copies, waits for them, and re-layouts  1.87 us (4%)
    pallas_call x1, Pallas kernels, step(): pl.pallas_call(lambda *refs: kernel(mesh, *refs), out_shape=jax.ShapeDtyp...  46.4 us
    unnamed x1, local copies, waits for them, and re-layouts  1.87 us

profile of v1, /device:TPU:0, one launch (start us, length us, event | category | flops | bytes accessed | tf_op | source)
XLA Modules:
  0.0 48.3 jit_solution(5125241835372833207)
XLA Ops:
  0.0 46.4 %attend.1 = bf16[32,32,256]{2,1,0:T(8,128)(2,1)} custom-call(bf16[32,32,256]{2,1,0:T(8,128)(2,1)} %refs_0_.1, bf16[32,2048,256]{2,1,0:T(8,128)(2,1)} %bitcast.2, bf16[32,2048,256]{2,1,0:T(8,128)(2,1)} %bitcast.3), custom_call_target="tpu_custom_call" | custom-call | tf_op jit(solution)/shard_map/attend/pallas_call | solution.py:194
  46.4 1.9 %copy.5 = bf16[32,32,256]{2,1,0:T(8,128)(2,1)} copy(bf16[32,32,256]{2,1,0:T(8,128)(2,1)} %attend.1) | data formatting | bytes 1048576

commit v2 on v0

v2 whole, which is shorter than its diff:
```python
import jax
import jax.numpy as jnp
from jax import lax
from jax.experimental import pallas as pl
from jax.experimental.pallas import tpu as pltpu
from jax.sharding import PartitionSpec as P

MESH = pl.DeviceIdType.MESH
GROUP = 4
SLOTS = 16
LEAD = 2
LOG2E = 1.4426950408889634
WEIGHTS = (LEAD + 1) * GROUP
COMM = {
    4: ((0, "core", 0),),
    5: ((1, "core", 0),),
    6: ((2, "core", 0),),
    7: ((3, "core", 0), (0, "chip", 0)),
    ("v", 21): ((4, "core", 0), (1, "chip", 0)),
    ("v", 23): ((2, "chip", 0),),
    ("v", 25): ((3, "chip", 0),),
    ("v", 26): ((5, "core", 0),),
    ("v", 28): ((4, "chip", 0),),
    ("v", 29): ((6, "core", 0),),
    "end": ((5, "chip", 0),),
    "end2": ((6, "chip", 0),),
}


def attend(q_hbm, k_hbm, v_hbm, o_ref, q_ref, kbuf, vbuf, scores, weights, mine, theirs, own, part, from_core, pair, from_chip, pair_last, chip_last, core_last,
           q_sem, k_sem, v_sem, mine_sem, theirs_sem, part_sem, core_sem, pair_sem, chip_sem, done_sem, out_sem, last_sem):
    count, heads, head = q_hbm.shape
    tokens = k_hbm.shape[1]
    groups = count // GROUP
    half = heads // 2
    last = count - GROUP
    factor = head**-0.5 * LOG2E

    dp, sp = lax.axis_index("dp"), lax.axis_index("sp")
    side = lax.rem(sp, 2)
    core = sp + 1 - 2 * side
    chip = lax.rem(sp + 2, 4)
    peers = (core, chip, lax.rem(core + 2, 4))
    rows = pl.ds(pl.multiple_of(side * half, half), half)
    other_rows = pl.ds(pl.multiple_of((1 - side) * half, half), half)

    def keys(s):
        return pltpu.make_async_copy(k_hbm.at[s], kbuf.at[s % SLOTS], k_sem.at[s % SLOTS])

    def values(s):
        return pltpu.make_async_copy(v_hbm.at[s], vbuf.at[s % SLOTS], v_sem.at[s % SLOTS])

    def remote(src, dst, send, recv, peer):
        return pltpu.make_async_remote_copy(src, dst, send, recv, device_id=(dp, peer), device_id_type=MESH)

    def stats(g, n):
        return remote(mine.at[g], theirs.at[g, n], mine_sem.at[g, n], theirs_sem.at[g, n], peers[n])

    def span(g):
        return pl.ds(GROUP * g, GROUP)

    def halves(g):
        return remote(part.at[span(g), other_rows], from_core.at[span(g)], part_sem.at[g], core_sem.at[g], core)

    def sums(g):
        return remote(pair.at[span(g)], from_chip.at[span(g)], pair_sem.at[g], chip_sem.at[g], chip)

    def results(g):
        return remote(o_ref.at[span(g), rows], o_ref.at[span(g), rows], done_sem.at[g], out_sem.at[g], core)

    def last_chip(j):
        return remote(part.at[last + j], chip_last.at[j], last_sem.at[0, j], last_sem.at[1, j], chip)

    def last_core(j):
        return remote(pair_last.at[j], core_last.at[j], last_sem.at[2, j], last_sem.at[3, j], core)

    def score(s):
        scores[s % GROUP] = lax.dot_general(
            q_ref[s], kbuf[s % SLOTS], (((1,), (1,)), ((), ())), preferred_element_type=jnp.float32
        )

    def softmax(s):
        x = scores[s % GROUP]
        high = jnp.max(x, 1, keepdims=True)
        w = jnp.exp2((x - high) * factor)
        weights[s % WEIGHTS] = w.astype(jnp.bfloat16)
        return high, jnp.sum(w, 1, keepdims=True)

    def gather(s, share):
        seen = jnp.dot(weights[s % WEIGHTS], vbuf[s % SLOTS], preferred_element_type=jnp.float32)
        seen = seen * share[:heads, s % GROUP : s % GROUP + 1]
        own[s] = seen
        part[s] = seen.astype(jnp.bfloat16)

    def keep_stats(g, pairs):
        lane = lax.broadcasted_iota(jnp.int32, (heads, 128), 1)
        x = jnp.zeros((heads, 128), jnp.float32)
        for j, (high, total) in enumerate(pairs):
            x = jnp.where(lane == j, high, x)
            x = jnp.where(lane == GROUP + j, total, x)
        mine[g, :, :heads] = x.T[: 2 * GROUP, :]

    def shares(g):
        for n in range(3):
            stats(g, n).wait_recv()
        rows = [mine[g]] + [theirs[g, n] for n in range(3)]
        highs, totals = [r[:GROUP] for r in rows], [r[GROUP:] for r in rows]
        top = jnp.maximum(jnp.maximum(highs[0], highs[1]), jnp.maximum(highs[2], highs[3]))
        scale = [jnp.exp2((h - top) * factor) for h in highs]
        parts = [t * s for t, s in zip(totals, scale)]
        whole = (parts[0] + parts[1]) + (parts[2] + parts[3])
        share = scale[0] / whole
        return jnp.concatenate([share, jnp.zeros_like(share)], 0).T

    def add_core(g):
        halves(g).wait_recv()
        pair[span(g)] = (own[span(g), rows] + from_core[span(g)].astype(jnp.float32)).astype(jnp.bfloat16)

    def add_chip(g):
        sums(g).wait_recv()
        o_ref[span(g), rows] = (pair[span(g)].astype(jnp.float32) + from_chip[span(g)].astype(jnp.float32)).astype(jnp.bfloat16)

    order = [("k", s) for s in range(LEAD * GROUP)]
    for s in range(count - (LEAD + 1) * GROUP):
        order += [("k", s + LEAD * GROUP), ("v", s)]
    order += [("k", s) for s in range(last, count)] + [("v", s) for s in range(count - (LEAD + 1) * GROUP, count)]

    def start(used_k, used_v):
        while order and order[0][1] < SLOTS + {"k": used_k, "v": used_v}[order[0][0]]:
            kind, s = order.pop(0)
            (keys if kind == "k" else values)(s).start(priority=1)

    pltpu.make_async_copy(q_hbm, q_ref, q_sem.at[0]).start()
    start(0, 0)
    barrier = pltpu.get_barrier_semaphore()
    for peer in peers:
        pl.semaphore_signal(barrier, inc=1, device_id=(dp, peer), device_id_type=MESH)
    pltpu.make_async_copy(q_hbm, q_ref, q_sem.at[0]).wait()

    for h in range(groups):
        g = h - LEAD
        paired = g >= 0 and h < groups - 1
        share = None
        if paired:
            for j in range(GROUP):
                keys(GROUP * h + j).wait()
                values(GROUP * g + j).wait()
            share = shares(g)
        sends = []
        for done, act, nxt in COMM.get(h, ()):
            (add_core if act == "core" else add_chip)(done)
            sends.append(sums(done) if act == "core" else results(done))
        pairs = []
        for j in range(GROUP):
            if not paired:
                keys(GROUP * h + j).wait()
            score(GROUP * h + j)
            if paired:
                gather(GROUP * g + j, share)
            pairs.append(softmax(GROUP * h + j))
        keep_stats(h, pairs)
        if h == 0:
            pl.semaphore_wait(barrier, 3)
        sends += [stats(h, n) for n in range(3)]
        if paired:
            sends.append(halves(g))
        for send in sends:
            send.start()
        start(GROUP * (h + 1), GROUP * (g + 1) if paired else 0 if g < 0 else GROUP * g)

    for s in range(count - (LEAD + 1) * GROUP, count):
        g, j = s // GROUP, s % GROUP
        if j == 0:
            share = shares(g)
        values(s).wait()
        gather(s, share)
        if g == groups - 1:
            last_chip(j).start()
        elif j == GROUP - 1:
            halves(g).start()
        for done, act, nxt in COMM.get(("v", s), ()):
            (add_core if act == "core" else add_chip)(done)
            (sums(done) if act == "core" else results(done)).start()

    for done, act, nxt in COMM["end"]:
        (add_core if act == "core" else add_chip)(done)
        (sums(done) if act == "core" else results(done)).start()
    for j in range(GROUP):
        last_chip(j).wait_recv()
        pair_last[j] = (part[last + j].astype(jnp.float32) + chip_last[j].astype(jnp.float32)).astype(jnp.bfloat16)
        last_core(j).start()
    for done, act, nxt in COMM["end2"]:
        (add_core if act == "core" else add_chip)(done)
        (sums(done) if act == "core" else results(done)).start()
    for j in range(GROUP):
        last_core(j).wait_recv()
        o_ref[last + j] = (pair_last[j].astype(jnp.float32) + core_last[j].astype(jnp.float32)).astype(jnp.bfloat16)
    for g in range(groups):
        for n in range(3):
            stats(g, n).wait_send()
    for g in range(groups - 1):
        halves(g).wait_send()
        sums(g).wait_send()
        results(g).wait()
    for j in range(GROUP):
        last_chip(j).wait_send()
        last_core(j).wait_send()


def solution(mesh):
    def step(q, k, v):
        count, heads, head = q.shape
        tokens = k.shape[1]
        groups = count // GROUP
        whole = (count, heads, head)
        dma = pltpu.SemaphoreType.DMA
        hbm = pl.BlockSpec(memory_space=pltpu.HBM)
        return pl.pallas_call(
            attend,
            out_shape=jax.ShapeDtypeStruct(whole, jnp.bfloat16),
            in_specs=[hbm] * 3,
            out_specs=pl.BlockSpec(memory_space=pltpu.VMEM),
            scratch_shapes=[
                pltpu.VMEM(whole, jnp.bfloat16),
                pltpu.VMEM((SLOTS, tokens, head), jnp.bfloat16),
                pltpu.VMEM((SLOTS, tokens, head), jnp.bfloat16),
                pltpu.VMEM((GROUP, heads, tokens), jnp.float32),
                pltpu.VMEM((WEIGHTS, heads, tokens), jnp.bfloat16),
                pltpu.VMEM((groups, 2 * GROUP, 128), jnp.float32),
                pltpu.VMEM((groups, 3, 2 * GROUP, 128), jnp.float32),
                pltpu.VMEM(whole, jnp.float32),
                pltpu.VMEM(whole, jnp.bfloat16),
                *[pltpu.VMEM((count, heads // 2, head), jnp.bfloat16)] * 3,
                *[pltpu.VMEM((GROUP, heads, head), jnp.bfloat16)] * 3,
                dma((1,)),
                dma((SLOTS,)),
                dma((SLOTS,)),
                dma((groups, 3)),
                dma((groups, 3)),
                *[dma((groups,))] * 6,
                dma((4, GROUP)),
            ],
            compiler_params=pltpu.CompilerParams(collective_id=0, has_side_effects=True, vmem_limit_bytes=44 * 2**20),
            name="attend",
        )(q, k.reshape(count, tokens, head), v.reshape(count, tokens, head))

    return jax.shard_map(
        step,
        mesh=mesh,
        in_specs=(P("dp", None, None), P("dp", "sp", None, None), P("dp", "sp", None, None)),
        out_specs=P("dp", None, None),
        check_vma=False,
    )
```

time: 134 us -> 36.2 us (0.27)
  waiting for transfers between devices: 46.6 us -> 0 us
  matrix products: 34.8 us -> 0 us
  Pallas kernels: 0 us -> 34.2 us
  other arithmetic: 19.4 us -> 0 us
  local copies, waits for them, and re-layouts: 19.1 us -> 1.84 us
  between operations: 13.4 us -> 0.01 us
    all_gather x1 -> x0, waiting for transfers between devices: 46.6 us -> none  [step(): return together(lax.all_gather(part_of(q, k, v), 'sp')).reshape(q.shape)]
    dot_general x2 -> x0, matrix products: 34.8 us -> none  [einsum(): return jnp.einsum(form, a.astype(jnp.float32), b.astype(jnp.float32))]
    pallas_call x0 -> x1, Pallas kernels: none -> 34.2 us  [step(): pl.pallas_call(attend, out_shape=jax.ShapeDtypeStruct(whole, jnp.bfloat16...]
    reduce_sum x3 -> x0, other arithmetic: 16.1 us -> none  [the longest x1 10.9 us: together(): jnp.sum(seen * scale, 0) / jnp.sum(total * scale, 0)]
    all_gather x1 -> x0, local copies, waits for them, and re-layouts: 14 us -> none  [step(): return together(lax.all_gather(part_of(q, k, v), 'sp')).reshape(q.shape)]
    reduce_sum x1 -> x0, local copies, waits for them, and re-layouts: 3.51 us -> none  [together(): jnp.sum(seen * scale, 0) / jnp.sum(total * scale, 0)]
    concatenate x1 -> x0, other arithmetic: 1.43 us -> none  [part_of(): jnp.concatenate([seen, jnp.sum(weights, -1, keepdims=True), high], -1)]
  transfers between devices with their start and end apart: 1 -> 0, of which waited for: 1 -> 0; matrix products, arithmetic and copies ran while one was open for 0% -> 0% of each run, Pallas kernels for 0% -> 0%
where the time goes in v2:
time: 36.2 us; the launch traced here: 36.1 us
  Pallas kernels  34.2 us (94%)
  local copies, waits for them, and re-layouts  1.84 us (5%)
    pallas_call x1, Pallas kernels, step(): pl.pallas_call(attend, out_shape=jax.ShapeDtypeStruct(whole, jnp.bfloat16...  34.2 us
    unnamed x3, local copies, waits for them, and re-layouts  1.84 us

profile of v2, /device:TPU:0, one launch (start us, length us, event | category | flops | bytes accessed | tf_op | source)
XLA Modules:
  0.0 36.1 jit_solution(3547810303956534592)
XLA Ops:
  0.0 0.0 copy-start
  0.0 1.0 %copy-done = bf16[32,32,256]{2,1,0:T(8,128)(2,1)S(1)} copy-done((bf16[32,32,256]{2,1,0:T(8,128)(2,1)S(1)}, bf16[32,32,256]{2,1,0:T(8,128)(2,1)}, u32[]{:S(2)}) %copy-start) | copy-done | bytes 524312
  1.0 34.2 %attend.1 = bf16[32,32,256]{2,1,0:T(8,128)(2,1)S(1)} custom-call(bf16[32,32,256]{2,1,0:T(8,128)(2,1)S(1)} %copy-done, bf16[32,2048,256]{2,1,0:T(8,128)(2,1)} %bitcast.2, bf16[32,2048,256]{2,1,0:T(8,128)(2,1)} %bitcast.3), custom_call_target="tpu_custom_call" | custom-call | tf_op jit(solution)/shard_map/attend/pallas_call | solution.py:218
  35.3 0.8 %copy.5 = bf16[32,32,256]{2,1,0:T(8,128)(2,1)} copy(bf16[32,32,256]{2,1,0:T(8,128)(2,1)S(1)} %attend.1) | data formatting | bytes 1048576
Async XLA Ops:
  0.0 1.0 %copy-start = (bf16[32,32,256]{2,1,0:T(8,128)(2,1)S(1)}, bf16[32,32,256]{2,1,0:T(8,128)(2,1)}, u32[]{:S(2)}) copy-start(bf16[32,32,256]{2,1,0:T(8,128)(2,1)} %q_hbm.1) | copy-start | bytes 1572868

commit v3 on v2

v3 whole, which is shorter than its diff:
```python
import jax
import jax.numpy as jnp
from jax import lax
from jax.experimental import pallas as pl
from jax.experimental.pallas import tpu as pltpu
from jax.sharding import PartitionSpec as P

MESH = pl.DeviceIdType.MESH
GROUP = 4
SLOTS = 32
LOG2E = 1.4426950408889634
BLOCKS = [range(4 * g, 4 * g + 4) for g in range(6)] + [range(24, 26), range(26, 28)] + [range(s, s + 1) for s in range(28, 32)]
SUMS = {
    1: (("core", 0),),
    2: (("core", 1),),
    3: (("core", 2),),
    4: (("chip", 0), ("core", 3)),
    5: (("chip", 1), ("core", 4)),
    7: (("chip", 2),),
    8: (("core", 5),),
    9: (("chip", 3),),
    11: (("core", 6), ("chip", 4)),
    "end": (("chip", 5),),
    "end2": (("chip", 6),),
}


def attend(q_hbm, k_hbm, v_hbm, o_ref, q_ref, buf, scores, weights, mine, theirs, own, part, from_core, pair, from_chip, pair_last, chip_last, core_last,
           q_sem, buf_sem, mine_sem, theirs_sem, part_sem, core_sem, pair_sem, chip_sem, done_sem, out_sem, last_sem):
    count, heads, head = q_hbm.shape
    tokens = k_hbm.shape[1]
    groups = count // GROUP
    half = heads // 2
    last = count - GROUP
    factor = head**-0.5 * LOG2E

    dp, sp = lax.axis_index("dp"), lax.axis_index("sp")
    side = lax.rem(sp, 2)
    core = sp + 1 - 2 * side
    chip = lax.rem(sp + 2, 4)
    peers = (core, chip, lax.rem(core + 2, 4))
    rows = pl.ds(pl.multiple_of(side * half, half), half)
    other_rows = pl.ds(pl.multiple_of((1 - side) * half, half), half)

    def keys(s):
        return pltpu.make_async_copy(k_hbm.at[s], buf.at[s % SLOTS], buf_sem.at[s % SLOTS])

    def values(s):
        n = count + s
        return pltpu.make_async_copy(v_hbm.at[s], buf.at[n % SLOTS], buf_sem.at[n % SLOTS])

    def remote(src, dst, send, recv, peer):
        return pltpu.make_async_remote_copy(src, dst, send, recv, device_id=(dp, peer), device_id_type=MESH)

    def stats(g, n):
        return remote(mine.at[g], theirs.at[g, n], mine_sem.at[g, n], theirs_sem.at[g, n], peers[n])

    def span(g):
        return pl.ds(GROUP * g, GROUP)

    def halves(g):
        return remote(part.at[span(g), other_rows], from_core.at[span(g)], part_sem.at[g], core_sem.at[g], core)

    def sums(g):
        return remote(pair.at[span(g)], from_chip.at[span(g)], pair_sem.at[g], chip_sem.at[g], chip)

    def results(g):
        return remote(o_ref.at[span(g), rows], o_ref.at[span(g), rows], done_sem.at[g], out_sem.at[g], core)

    def last_chip(j):
        return remote(part.at[last + j], chip_last.at[j], last_sem.at[0, j], last_sem.at[1, j], chip)

    def last_core(j):
        return remote(pair_last.at[j], core_last.at[j], last_sem.at[2, j], last_sem.at[3, j], core)

    def score(s):
        scores[s % GROUP] = lax.dot_general(
            q_ref[s], buf[s % SLOTS], (((1,), (1,)), ((), ())), preferred_element_type=jnp.float32
        )

    def softmax(s):
        x = scores[s % GROUP]
        high = jnp.max(x, 1, keepdims=True)
        w = jnp.exp2((x - high) * factor)
        weights[s] = w.astype(jnp.bfloat16)
        return high, jnp.sum(w, 1, keepdims=True)

    def gather(s, share):
        n = (count + s) % SLOTS
        seen = [jnp.dot(weights[s], buf[n, :, c : c + 128], preferred_element_type=jnp.float32) for c in range(0, head, 128)]
        seen = jnp.concatenate(seen, 1) * share[:heads, s % GROUP : s % GROUP + 1]
        own[s] = seen
        part[s] = seen.astype(jnp.bfloat16)

    def keep_stats(g, pairs):
        lane = lax.broadcasted_iota(jnp.int32, (heads, 128), 1)
        x = jnp.zeros((heads, 128), jnp.float32)
        for j, (high, total) in enumerate(pairs):
            x = jnp.where(lane == j, high, x)
            x = jnp.where(lane == GROUP + j, total, x)
        mine[g, :, :heads] = x.T[: 2 * GROUP, :]

    def shares(g):
        for n in range(3):
            stats(g, n).wait_recv()
        rows = [mine[g]] + [theirs[g, n] for n in range(3)]
        highs, totals = [r[:GROUP] for r in rows], [r[GROUP:] for r in rows]
        top = jnp.maximum(jnp.maximum(highs[0], highs[1]), jnp.maximum(highs[2], highs[3]))
        scale = [jnp.exp2((h - top) * factor) for h in highs]
        parts = [t * s for t, s in zip(totals, scale)]
        whole = (parts[0] + parts[1]) + (parts[2] + parts[3])
        share = scale[0] / whole
        return jnp.concatenate([share, jnp.zeros_like(share)], 0).T

    def add_core(g):
        halves(g).wait_recv()
        pair[span(g)] = (own[span(g), rows] + from_core[span(g)].astype(jnp.float32)).astype(jnp.bfloat16)

    def add_chip(g):
        sums(g).wait_recv()
        o_ref[span(g), rows] = (pair[span(g)].astype(jnp.float32) + from_chip[span(g)].astype(jnp.float32)).astype(jnp.bfloat16)

    def sum_parts(step):
        for over, g in SUMS.get(step, ()):
            if over == "core":
                add_core(g)
                sums(g).start()
            else:
                add_chip(g)
                results(g).start()

    pltpu.make_async_copy(q_hbm, q_ref, q_sem.at[0]).start()
    for n in range(SLOTS):
        keys(n).start(priority=1)
    barrier = pltpu.get_barrier_semaphore()
    for peer in peers:
        pl.semaphore_signal(barrier, inc=1, device_id=(dp, peer), device_id_type=MESH)
    pltpu.make_async_copy(q_hbm, q_ref, q_sem.at[0]).wait()

    pairs = []

    def send_stats(g):
        keep_stats(g, [pairs.pop(0) for _ in range(GROUP)])
        if g == 0:
            pl.semaphore_wait(barrier, 3)
        for n in range(3):
            stats(g, n).start()

    for g in range(groups):
        for s in range(GROUP * g, GROUP * g + GROUP):
            keys(s).wait()
        for s in range(GROUP * g, GROUP * g + GROUP):
            score(s)
            if s:
                pairs.append(softmax(s - 1))
        if g:
            send_stats(g - 1)
        for s in range(GROUP * g, GROUP * g + GROUP):
            values(s).start(priority=1)
    pairs.append(softmax(count - 1))
    send_stats(groups - 1)

    for step, block in enumerate(BLOCKS):
        for s in block:
            values(s).wait()
        g = block[0] // GROUP
        if block[0] % GROUP == 0:
            share = shares(g)
        for s in block:
            gather(s, share)
        if g == groups - 1:
            last_chip(block[0] % GROUP).start()
        elif block[-1] % GROUP == GROUP - 1:
            halves(g).start()
        sum_parts(step)

    sum_parts("end")
    for j in range(GROUP):
        last_chip(j).wait_recv()
        pair_last[j] = (part[last + j].astype(jnp.float32) + chip_last[j].astype(jnp.float32)).astype(jnp.bfloat16)
        last_core(j).start()
    sum_parts("end2")
    for j in range(GROUP):
        last_core(j).wait_recv()
        o_ref[last + j] = (pair_last[j].astype(jnp.float32) + core_last[j].astype(jnp.float32)).astype(jnp.bfloat16)
    for g in range(groups):
        for n in range(3):
            stats(g, n).wait_send()
    for g in range(groups - 1):
        halves(g).wait_send()
        sums(g).wait_send()
        results(g).wait()
    for j in range(GROUP):
        last_chip(j).wait_send()
        last_core(j).wait_send()


def solution(mesh):
    def step(q, k, v):
        count, heads, head = q.shape
        tokens = k.shape[1]
        groups = count // GROUP
        whole = (count, heads, head)
        dma = pltpu.SemaphoreType.DMA
        hbm = pl.BlockSpec(memory_space=pltpu.HBM)
        return pl.pallas_call(
            attend,
            out_shape=jax.ShapeDtypeStruct(whole, jnp.bfloat16),
            in_specs=[hbm] * 3,
            out_specs=pl.BlockSpec(memory_space=pltpu.VMEM),
            scratch_shapes=[
                pltpu.VMEM(whole, jnp.bfloat16),
                pltpu.VMEM((SLOTS, tokens, head), jnp.bfloat16),
                pltpu.VMEM((GROUP, heads, tokens), jnp.float32),
                pltpu.VMEM((count, heads, tokens), jnp.bfloat16),
                pltpu.VMEM((groups, 2 * GROUP, 128), jnp.float32),
                pltpu.VMEM((groups, 3, 2 * GROUP, 128), jnp.float32),
                pltpu.VMEM(whole, jnp.float32),
                pltpu.VMEM(whole, jnp.bfloat16),
                *[pltpu.VMEM((count, heads // 2, head), jnp.bfloat16)] * 3,
                *[pltpu.VMEM((GROUP, heads, head), jnp.bfloat16)] * 3,
                dma((1,)),
                dma((SLOTS,)),
                dma((groups, 3)),
                dma((groups, 3)),
                *[dma((groups,))] * 6,
                dma((4, GROUP)),
            ],
            compiler_params=pltpu.CompilerParams(collective_id=0, has_side_effects=True, vmem_limit_bytes=48 * 2**20),
            name="attend",
        )(q, k.reshape(count, tokens, head), v.reshape(count, tokens, head))

    return jax.shard_map(
        step,
        mesh=mesh,
        in_specs=(P("dp", None, None), P("dp", "sp", None, None), P("dp", "sp", None, None)),
        out_specs=P("dp", None, None),
        check_vma=False,
    )
```

time: 36.2 us -> 31.2 us (0.86)
  Pallas kernels: 34.2 us -> 29.2 us
    pallas_call x1, Pallas kernels: 34.2 us -> 29.2 us  [step(): pl.pallas_call(attend, out_shape=jax.ShapeDtypeStruct(whole, jnp.bfloat16...]
where the time goes in v3:
time: 31.2 us; the launch traced here: 31 us
  Pallas kernels  29.2 us (94%)
  local copies, waits for them, and re-layouts  1.84 us (6%)
    pallas_call x1, Pallas kernels, step(): pl.pallas_call(attend, out_shape=jax.ShapeDtypeStruct(whole, jnp.bfloat16...  29.2 us
    unnamed x3, local copies, waits for them, and re-layouts  1.84 us

profile of v3, /device:TPU:0, one launch (start us, length us, event | category | flops | bytes accessed | tf_op | source)
XLA Modules:
  0.0 31.0 jit_solution(7690128108849952950)
XLA Ops:
  0.0 0.0 copy-start
  0.0 1.0 %copy-done = bf16[32,32,256]{2,1,0:T(8,128)(2,1)S(1)} copy-done((bf16[32,32,256]{2,1,0:T(8,128)(2,1)S(1)}, bf16[32,32,256]{2,1,0:T(8,128)(2,1)}, u32[]{:S(2)}) %copy-start) | copy-done | bytes 524312
  1.0 29.2 %attend.1 = bf16[32,32,256]{2,1,0:T(8,128)(2,1)S(1)} custom-call(bf16[32,32,256]{2,1,0:T(8,128)(2,1)S(1)} %copy-done, bf16[32,2048,256]{2,1,0:T(8,128)(2,1)} %bitcast.2, bf16[32,2048,256]{2,1,0:T(8,128)(2,1)} %bitcast.3), custom_call_target="tpu_custom_call" | custom-call | tf_op jit(solution)/shard_map/attend/pallas_call | solution.py:206
  30.2 0.8 %copy.5 = bf16[32,32,256]{2,1,0:T(8,128)(2,1)} copy(bf16[32,32,256]{2,1,0:T(8,128)(2,1)S(1)} %attend.1) | data formatting | bytes 1048576
Async XLA Ops:
  0.0 1.0 %copy-start = (bf16[32,32,256]{2,1,0:T(8,128)(2,1)S(1)}, bf16[32,32,256]{2,1,0:T(8,128)(2,1)}, u32[]{:S(2)}) copy-start(bf16[32,32,256]{2,1,0:T(8,128)(2,1)} %q_hbm.1) | copy-start | bytes 1572868

commit v4 on v0

v4 whole, which is shorter than its diff:
```python
import jax
import jax.numpy as jnp
from jax import lax
from jax.experimental import pallas as pl
from jax.experimental.pallas import tpu as pltpu
from jax.sharding import PartitionSpec as P

MESH = pl.DeviceIdType.MESH
LOG2E = 1.4426950408889634
SLOTS = 32
READS = 14
STATS = 8
SCORES = 4

BLOCKS = (
    [("k", s, 4) for s in (0, 4, 8, 12, 16)]
    + [("v", 0, 4), ("k", 20, 4), ("v", 4, 4), ("k", 24, 4), ("v", 8, 4), ("k", 28, 4), ("v", 12, 4), ("v", 16, 4)]
    + [("v", s, 2) for s in (20, 22, 24, 26)]
    + [("v", s, 1) for s in (28, 29, 30, 31)]
)
SPANS = [(s, n) for kind, s, n in BLOCKS if kind == "v" and s < 28]
LATE = (28, 29, 30)
FINAL = 31
SUMS = {
    6: ("core0",),
    8: ("core1",),
    9: ("chip0",),
    10: ("core2",),
    11: ("chip1",),
    12: ("core3",),
    13: ("chip2",),
    15: ("core4", "core5"),
    16: ("core6",),
    18: ("core7",),
    20: ("core8", "chip3"),
}
DRAIN = ("chip4", "chip5", "chip6", "late0", "late1", "chip7", "late2", "final", "chip8")


def attend(q_hbm, k_hbm, v_hbm, o_ref, q_ref, buf, scores, weights, mine, theirs, own, part, from_core, pair, from_chip, late_pair, late_chip, late_core, final_in,
           q_sem, buf_sem, stats_out, stats_in, core_out, core_in, chip_out, chip_in, done_out, done_in, late_out, late_chip_in, late_core_in, final_sem):
    count, heads, head = q_hbm.shape
    half = heads // 2
    factor = head**-0.5 * LOG2E

    dp, sp = lax.axis_index("dp"), lax.axis_index("sp")
    side = lax.rem(sp, 2)
    core = sp + 1 - 2 * side
    chip = lax.rem(sp + 2, 4)
    peers = (core, chip, lax.rem(core + 2, 4))
    rows = pl.ds(pl.multiple_of(side * half, half), half)
    other_rows = pl.ds(pl.multiple_of((1 - side) * half, half), half)

    first = [sum(n for _, _, n in BLOCKS[:b]) for b in range(len(BLOCKS))]
    slot_of = {(kind, s + i): (first[b] + i) % SLOTS for b, (kind, s, n) in enumerate(BLOCKS) for i in range(n)}

    def read(b):
        kind, s, n = BLOCKS[b]
        src = k_hbm if kind == "k" else v_hbm
        return pltpu.make_async_copy(src.at[pl.ds(s, n)], buf.at[pl.ds(first[b] % SLOTS, n)], buf_sem.at[b % READS])

    def remote(src, dst, send, recv, peer):
        return pltpu.make_async_remote_copy(src, dst, send, recv, device_id=(dp, peer), device_id_type=MESH)

    def stats(g, n):
        return remote(mine.at[g], theirs.at[g, n], stats_out, stats_in.at[g], peers[n])

    def span(c):
        return pl.ds(*SPANS[c])

    def halves(c):
        return remote(part.at[span(c), other_rows], from_core.at[span(c)], core_out, core_in.at[c], core)

    def sums(c):
        return remote(pair.at[span(c)], from_chip.at[span(c)], chip_out, chip_in.at[c], chip)

    def results(c):
        return remote(o_ref.at[span(c), rows], o_ref.at[span(c), rows], done_out, done_in, core)

    def to_chip(i):
        return remote(part.at[LATE[i]], late_chip.at[i], late_out, late_chip_in.at[i], chip)

    def to_core(i):
        return remote(late_pair.at[i], late_core.at[i], late_out, late_core_in.at[i], core)

    def to_all(n):
        return remote(part.at[FINAL], final_in.at[n], late_out, final_sem, peers[n])

    def add(a, b):
        return a.astype(jnp.float32) + b.astype(jnp.float32)

    def score(s):
        scores[s % SCORES] = lax.dot_general(
            q_ref[s], buf[slot_of["k", s]], (((1,), (1,)), ((), ())), preferred_element_type=jnp.float32
        )

    def softmax(s):
        x = scores[s % SCORES]
        high = jnp.max(x, 1, keepdims=True)
        w = jnp.exp2((x - high) * factor)
        weights[s] = w.astype(jnp.bfloat16)
        return high, jnp.sum(w, 1, keepdims=True)

    def gather(s, share):
        v = slot_of["v", s]
        seen = [jnp.dot(weights[s], buf[v, :, c : c + 128], preferred_element_type=jnp.float32) for c in range(0, head, 128)]
        seen = jnp.concatenate(seen, 1) * share[:heads, s % STATS : s % STATS + 1]
        own[s] = seen
        part[s] = seen.astype(jnp.bfloat16)

    def send_stats(g, pairs):
        lane = lax.broadcasted_iota(jnp.int32, (heads, 128), 1)
        x = jnp.zeros((heads, 128), jnp.float32)
        for j, (high, total) in enumerate(pairs):
            x = jnp.where(lane == j, high, x)
            x = jnp.where(lane == STATS + j, total, x)
        mine[g, :, :heads] = x.T[: 2 * STATS, :]
        for n in range(3):
            stats(g, n).start()

    def shares(g):
        remote(theirs.at[g], theirs.at[g], stats_out, stats_in.at[g], core).wait_recv()
        rows = [mine[g]] + [theirs[g, n] for n in range(3)]
        highs, totals = [r[:STATS] for r in rows], [r[STATS:] for r in rows]
        top = jnp.maximum(jnp.maximum(highs[0], highs[1]), jnp.maximum(highs[2], highs[3]))
        scale = [jnp.exp2((h - top) * factor) for h in highs]
        parts = [t * s for t, s in zip(totals, scale)]
        whole = (parts[0] + parts[1]) + (parts[2] + parts[3])
        return (scale[0] / whole).T

    def sum_parts(what):
        kind, i = what.rstrip("0123456789"), int("0" + what.lstrip("abcdefghijklmnopqrstuvwxyz"))
        if kind == "core":
            halves(i).wait_recv()
            pair[span(i)] = add(own[span(i), rows], from_core[span(i)]).astype(jnp.bfloat16)
            sums(i).start()
        elif kind == "chip":
            sums(i).wait_recv()
            o_ref[span(i), rows] = add(pair[span(i)], from_chip[span(i)]).astype(jnp.bfloat16)
            results(i).start()
        elif kind == "late":
            to_chip(i).wait_recv()
            late_pair[i] = add(part[LATE[i]], late_chip[i]).astype(jnp.bfloat16)
            to_core(i).start()
        else:
            remote(final_in, final_in, late_out, final_sem, core).wait_recv()
            o_ref[FINAL] = (add(part[FINAL], final_in[0]) + add(final_in[1], final_in[2])).astype(jnp.bfloat16)

    pltpu.make_async_copy(q_hbm, q_ref, q_sem).start()
    reads = list(range(len(BLOCKS)))

    def start_reads(used):
        while reads and first[reads[0]] + BLOCKS[reads[0]][2] <= SLOTS + used:
            read(reads.pop(0)).start(priority=1)

    start_reads(0)
    barrier = pltpu.get_barrier_semaphore()
    for peer in peers:
        pl.semaphore_signal(barrier, inc=1, device_id=(dp, peer), device_id_type=MESH)
    pltpu.make_async_copy(q_hbm, q_ref, q_sem).wait()

    waiting, pairs, group, share = [], [], 0, {}
    for b, (kind, lo, n) in enumerate(BLOCKS):
        read(b).wait()
        if kind == "v" and lo % STATS == 0:
            share = shares(lo // STATS)
        for s in range(lo, lo + n):
            if kind == "k":
                score(s)
            else:
                gather(s, share)
            if waiting:
                pairs.append(softmax(waiting.pop(0)))
            if kind == "k":
                waiting.append(s)
        if len(pairs) >= STATS:
            if group == 0:
                pl.semaphore_wait(barrier, 3)
            send_stats(group, pairs[:STATS])
            pairs, group = pairs[STATS:], group + 1
        if kind == "v":
            if (lo, n) in SPANS:
                halves(SPANS.index((lo, n))).start()
            elif lo in LATE:
                to_chip(LATE.index(lo)).start()
        for what in SUMS.get(b, ()):
            sum_parts(what)
        if kind == "v" and lo == FINAL:
            for i in (1, 2, 0):
                to_all(i).start()
        start_reads(first[b] + n)

    for what in DRAIN:
        sum_parts(what)
    for i, s in enumerate(LATE):
        to_core(i).wait_recv()
        o_ref[s] = add(late_pair[i], late_core[i]).astype(jnp.bfloat16)

    summed = from_core.at[pl.ds(0, LATE[0])]
    remote(summed, summed, done_out, done_in, core).wait()
    remote(summed, summed, core_out, done_in, core).wait_send()
    remote(summed, summed, chip_out, done_in, core).wait_send()
    remote(theirs, theirs, stats_out, done_in, core).wait_send()
    sent = part.at[pl.ds(0, 2 * len(LATE) + 3)]
    remote(sent, sent, late_out, done_in, core).wait_send()


def solution(mesh):
    def step(q, k, v):
        count, heads, head = q.shape
        tokens = k.shape[1]
        whole = (count, heads, head)
        dma = pltpu.SemaphoreType.DMA
        hbm = pl.BlockSpec(memory_space=pltpu.HBM)
        return pl.pallas_call(
            attend,
            out_shape=jax.ShapeDtypeStruct(whole, jnp.bfloat16),
            in_specs=[hbm] * 3,
            out_specs=pl.BlockSpec(memory_space=pltpu.VMEM),
            scratch_shapes=[
                pltpu.VMEM(whole, jnp.bfloat16),
                pltpu.VMEM((SLOTS, tokens, head), jnp.bfloat16),
                pltpu.VMEM((SCORES, heads, tokens), jnp.float32),
                pltpu.VMEM((count, heads, tokens), jnp.bfloat16),
                pltpu.VMEM((count // STATS, 2 * STATS, 128), jnp.float32),
                pltpu.VMEM((count // STATS, 3, 2 * STATS, 128), jnp.float32),
                pltpu.VMEM(whole, jnp.float32),
                pltpu.VMEM(whole, jnp.bfloat16),
                *[pltpu.VMEM((count, heads // 2, head), jnp.bfloat16)] * 3,
                *[pltpu.VMEM((len(LATE), heads, head), jnp.bfloat16)] * 3,
                pltpu.VMEM((3, heads, head), jnp.bfloat16),
                dma,
                dma((READS,)),
                dma,
                dma((count // STATS,)),
                dma,
                dma((len(SPANS),)),
                dma,
                dma((len(SPANS),)),
                dma,
                dma,
                dma,
                dma((len(LATE),)),
                dma((len(LATE),)),
                dma,
            ],
            compiler_params=pltpu.CompilerParams(collective_id=0, has_side_effects=True, vmem_limit_bytes=48 * 2**20),
            name="attend",
        )(pltpu.with_memory_space_constraint(q, pltpu.HBM), k.reshape(count, tokens, head), v.reshape(count, tokens, head))

    return jax.shard_map(
        step,
        mesh=mesh,
        in_specs=(P("dp", None, None), P("dp", "sp", None, None), P("dp", "sp", None, None)),
        out_specs=P("dp", None, None),
        check_vma=False,
    )
```

time: 134 us -> 29.7 us (0.22)
  waiting for transfers between devices: 46.6 us -> 0 us
  matrix products: 34.8 us -> 0 us
  Pallas kernels: 0 us -> 28.8 us
  other arithmetic: 19.4 us -> 0 us
  local copies, waits for them, and re-layouts: 19.1 us -> 0.8 us
  between operations: 13.4 us -> 0.01 us
    all_gather x1 -> x0, waiting for transfers between devices: 46.6 us -> none  [step(): return together(lax.all_gather(part_of(q, k, v), 'sp')).reshape(q.shape)]
    dot_general x2 -> x0, matrix products: 34.8 us -> none  [einsum(): return jnp.einsum(form, a.astype(jnp.float32), b.astype(jnp.float32))]
    pallas_call x0 -> x1, Pallas kernels: none -> 28.8 us  [step(): pl.pallas_call(attend, out_shape=jax.ShapeDtypeStruct(whole, jnp.bfloat16...]
    reduce_sum x3 -> x0, other arithmetic: 16.1 us -> none  [the longest x1 10.9 us: together(): jnp.sum(seen * scale, 0) / jnp.sum(total * scale, 0)]
    all_gather x1 -> x0, local copies, waits for them, and re-layouts: 14 us -> none  [step(): return together(lax.all_gather(part_of(q, k, v), 'sp')).reshape(q.shape)]
    reduce_sum x1 -> x0, local copies, waits for them, and re-layouts: 3.51 us -> none  [together(): jnp.sum(seen * scale, 0) / jnp.sum(total * scale, 0)]
    concatenate x1 -> x0, other arithmetic: 1.43 us -> none  [part_of(): jnp.concatenate([seen, jnp.sum(weights, -1, keepdims=True), high], -1)]
  transfers between devices with their start and end apart: 1 -> 0, of which waited for: 1 -> 0; matrix products, arithmetic and copies ran while one was open for 0% -> 0% of each run, Pallas kernels for 0% -> 0%
where the time goes in v4:
time: 29.7 us; the launch traced here: 29.6 us
  Pallas kernels  28.8 us (97%)
  local copies, waits for them, and re-layouts  0.8 us (3%)
    pallas_call x1, Pallas kernels, step(): pl.pallas_call(attend, out_shape=jax.ShapeDtypeStruct(whole, jnp.bfloat16...  28.8 us
    unnamed x1, local copies, waits for them, and re-layouts  0.8 us

profile of v4, /device:TPU:0, one launch (start us, length us, event | category | flops | bytes accessed | tf_op | source)
XLA Modules:
  0.0 29.6 jit_solution(2692849733624039857)
XLA Ops:
  0.0 28.8 %attend.1 = bf16[32,32,256]{2,1,0:T(8,128)(2,1)S(1)} custom-call(bf16[32,32,256]{2,1,0:T(8,128)(2,1)} %q_hbm.1, bf16[32,2048,256]{2,1,0:T(8,128)(2,1)} %bitcast.2, bf16[32,2048,256]{2,1,0:T(8,128)(2,1)} %bitcast.3), custom_call_target="tpu_custom_call" | custom-call | tf_op jit(solution)/shard_map/attend/pallas_call | solution.py:215
  28.8 0.8 %copy.5 = bf16[32,32,256]{2,1,0:T(8,128)(2,1)} copy(bf16[32,32,256]{2,1,0:T(8,128)(2,1)S(1)} %attend.1) | data formatting | bytes 1048576

commit v5 on v4

--- a/solution.py
+++ b/solution.py
@@ -8,34 +8,53 @@
 MESH = pl.DeviceIdType.MESH
 LOG2E = 1.4426950408889634
 SLOTS = 32
-READS = 14
+READS = 8
+BYROWS = 24
 STATS = 8
 SCORES = 4
 
 BLOCKS = (
-    [("k", s, 4) for s in (0, 4, 8, 12, 16)]
-    + [("v", 0, 4), ("k", 20, 4), ("v", 4, 4), ("k", 24, 4), ("v", 8, 4), ("k", 28, 4), ("v", 12, 4), ("v", 16, 4)]
-    + [("v", s, 2) for s in (20, 22, 24, 26)]
-    + [("v", s, 1) for s in (28, 29, 30, 31)]
+    ("k", 0, 4),
+    ("k", 4, 4),
+    ("k", 8, 4),
+    ("k", 12, 4),
+    ("k", 16, 4),
+    ("k", 20, 4),
+    ("k", 24, 4),
+    ("k", 28, 4),
+    ("v", 0, 4),
+    ("v", 4, 4),
+    ("v", 8, 4),
+    ("v", 12, 4),
+    ("v", 16, 2),
+    ("v", 18, 2),
+    ("v", 20, 2),
+    ("v", 22, 2),
+    ("v", 24, 1),
+    ("v", 25, 1),
+    ("v", 26, 1),
+    ("v", 27, 1),
+    ("v", 28, 1),
+    ("v", 29, 1),
+    ("v", 30, 1),
+    ("v", 31, 1),
 )
-SPANS = [(s, n) for kind, s, n in BLOCKS if kind == "v" and s < 28]
-LATE = (28, 29, 30)
-FINAL = 31
+LATE = (29, 30)
+FINAL = (31,)
+SPANS = ((0, 8), (8, 8), (16, 4), (20, 4), (24, 1), (25, 1), (26, 1), (27, 1), (28, 1))
 SUMS = {
-    6: ("core0",),
-    8: ("core1",),
-    9: ("chip0",),
-    10: ("core2",),
-    11: ("chip1",),
-    12: ("core3",),
-    13: ("chip2",),
-    15: ("core4", "core5"),
-    16: ("core6",),
-    18: ("core7",),
-    20: ("core8", "chip3"),
+    10: ("core0",),
+    13: ("core1",),
+    15: ("core2",),
+    16: ("chip0",),
+    18: ("core3",),
+    19: ("core4",),
+    20: ("core5",),
+    21: ("core6",),
+    22: ("core7",),
+    23: ("core8", "chip1"),
 }
-DRAIN = ("chip4", "chip5", "chip6", "late0", "late1", "chip7", "late2", "final", "chip8")
-
+DRAIN = ("chip2", "chip3", "chip4", "chip5", "chip6", "late0", "chip7", "late1", "chip8", "final0")
 
 def attend(q_hbm, k_hbm, v_hbm, o_ref, q_ref, buf, scores, weights, mine, theirs, own, part, from_core, pair, from_chip, late_pair, late_chip, late_core, final_in,
            q_sem, buf_sem, stats_out, stats_in, core_out, core_in, chip_out, chip_in, done_out, done_in, late_out, late_chip_in, late_core_in, final_sem):
@@ -83,8 +102,8 @@
     def to_core(i):
         return remote(late_pair.at[i], late_core.at[i], late_out, late_core_in.at[i], core)
 
-    def to_all(n):
-        return remote(part.at[FINAL], final_in.at[n], late_out, final_sem, peers[n])
+    def to_all(i, n):
+        return remote(part.at[FINAL[i]], final_in.at[i, n], late_out, final_sem.at[i], peers[n])
 
     def add(a, b):
         return a.astype(jnp.float32) + b.astype(jnp.float32)
@@ -103,8 +122,14 @@
 
     def gather(s, share):
         v = slot_of["v", s]
-        seen = [jnp.dot(weights[s], buf[v, :, c : c + 128], preferred_element_type=jnp.float32) for c in range(0, head, 128)]
-        seen = jnp.concatenate(seen, 1) * share[:heads, s % STATS : s % STATS + 1]
+        share = share[:heads, s % STATS : s % STATS + 1]
+        if s < BYROWS:
+            seen = [jnp.dot(weights[s], buf[v, :, c : c + 128], preferred_element_type=jnp.float32) for c in range(0, head, 128)]
+            seen = jnp.concatenate(seen, 1) * share
+        else:
+            cut = buf.shape[1] // 2
+            seen = [jnp.dot(weights[s, :, c : c + cut], buf[v, c : c + cut], preferred_element_type=jnp.float32) * share for c in (0, cut)]
+            seen = seen[0] + seen[1]
         own[s] = seen
         part[s] = seen.astype(jnp.bfloat16)
 
@@ -143,17 +168,17 @@
             late_pair[i] = add(part[LATE[i]], late_chip[i]).astype(jnp.bfloat16)
             to_core(i).start()
         else:
-            remote(final_in, final_in, late_out, final_sem, core).wait_recv()
-            o_ref[FINAL] = (add(part[FINAL], final_in[0]) + add(final_in[1], final_in[2])).astype(jnp.bfloat16)
+            remote(final_in.at[i], final_in.at[i], late_out, final_sem.at[i], core).wait_recv()
+            o_ref[FINAL[i]] = (add(part[FINAL[i]], final_in[i, 0]) + add(final_in[i, 1], final_in[i, 2])).astype(jnp.bfloat16)
 
     pltpu.make_async_copy(q_hbm, q_ref, q_sem).start()
     reads = list(range(len(BLOCKS)))
 
-    def start_reads(used):
-        while reads and first[reads[0]] + BLOCKS[reads[0]][2] <= SLOTS + used:
+    def start_reads(done, used):
+        while reads and reads[0] < READS + done and first[reads[0]] + BLOCKS[reads[0]][2] <= SLOTS + used:
             read(reads.pop(0)).start(priority=1)
 
-    start_reads(0)
+    start_reads(0, 0)
     barrier = pltpu.get_barrier_semaphore()
     for peer in peers:
         pl.semaphore_signal(barrier, inc=1, device_id=(dp, peer), device_id_type=MESH)
@@ -179,16 +204,17 @@
             send_stats(group, pairs[:STATS])
             pairs, group = pairs[STATS:], group + 1
         if kind == "v":
-            if (lo, n) in SPANS:
-                halves(SPANS.index((lo, n))).start()
-            elif lo in LATE:
+            for c, (s, m) in enumerate(SPANS):
+                if s + m == lo + n:
+                    halves(c).start()
+            if lo in LATE:
                 to_chip(LATE.index(lo)).start()
         for what in SUMS.get(b, ()):
             sum_parts(what)
-        if kind == "v" and lo == FINAL:
-            for i in (1, 2, 0):
-                to_all(i).start()
-        start_reads(first[b] + n)
+        if kind == "v" and lo in FINAL:
+            for peer in (1, 2, 0):
+                to_all(FINAL.index(lo), peer).start()
+        start_reads(b + 1, first[b] + n)
 
     for what in DRAIN:
         sum_parts(what)
@@ -196,12 +222,12 @@
         to_core(i).wait_recv()
         o_ref[s] = add(late_pair[i], late_core[i]).astype(jnp.bfloat16)
 
-    summed = from_core.at[pl.ds(0, LATE[0])]
+    summed = from_core.at[pl.ds(0, sum(n for _, n in SPANS))]
     remote(summed, summed, done_out, done_in, core).wait()
     remote(summed, summed, core_out, done_in, core).wait_send()
     remote(summed, summed, chip_out, done_in, core).wait_send()
     remote(theirs, theirs, stats_out, done_in, core).wait_send()
-    sent = part.at[pl.ds(0, 2 * len(LATE) + 3)]
+    sent = part.at[pl.ds(0, 2 * len(LATE) + 3 * len(FINAL))]
     remote(sent, sent, late_out, done_in, core).wait_send()
 
 
@@ -228,7 +254,7 @@
                 pltpu.VMEM(whole, jnp.bfloat16),
                 *[pltpu.VMEM((count, heads // 2, head), jnp.bfloat16)] * 3,
                 *[pltpu.VMEM((len(LATE), heads, head), jnp.bfloat16)] * 3,
-                pltpu.VMEM((3, heads, head), jnp.bfloat16),
+                pltpu.VMEM((len(FINAL), 3, heads, head), jnp.bfloat16),
                 dma,
                 dma((READS,)),
                 dma,
@@ -242,7 +268,7 @@
                 dma,
                 dma((len(LATE),)),
                 dma((len(LATE),)),
-                dma,
+                dma((len(FINAL),)),
             ],
             compiler_params=pltpu.CompilerParams(collective_id=0, has_side_effects=True, vmem_limit_bytes=48 * 2**20),
             name="attend",

time: 29.7 us -> 28.6 us (0.963)
  Pallas kernels: 28.8 us -> 27.7 us
    pallas_call x1, Pallas kernels: 28.8 us -> 27.7 us  [step(): pl.pallas_call(attend, out_shape=jax.ShapeDtypeStruct(whole, jnp.bfloat16...]
where the time goes in v5:
time: 28.6 us
  Pallas kernels  27.7 us (97%)
  local copies, waits for them, and re-layouts  0.8 us (3%)
    pallas_call x1, Pallas kernels, step(): pl.pallas_call(attend, out_shape=jax.ShapeDtypeStruct(whole, jnp.bfloat16...  27.7 us
    unnamed x1, local copies, waits for them, and re-layouts  0.8 us

profile of v5, /device:TPU:0, one launch (start us, length us, event | category | flops | bytes accessed | tf_op | source)
XLA Modules:
  0.0 28.6 jit_solution(11795898119200765104)
XLA Ops:
  0.0 27.7 %attend.1 = bf16[32,32,256]{2,1,0:T(8,128)(2,1)S(1)} custom-call(bf16[32,32,256]{2,1,0:T(8,128)(2,1)} %q_hbm.1, bf16[32,2048,256]{2,1,0:T(8,128)(2,1)} %bitcast.2, bf16[32,2048,256]{2,1,0:T(8,128)(2,1)} %bitcast.3), custom_call_target="tpu_custom_call" | custom-call | tf_op jit(solution)/shard_map/attend/pallas_call | solution.py:241
  27.8 0.8 %copy.5 = bf16[32,32,256]{2,1,0:T(8,128)(2,1)} copy(bf16[32,32,256]{2,1,0:T(8,128)(2,1)S(1)} %attend.1) | data formatting | bytes 1048576

commit v6 on v5

--- a/solution.py
+++ b/solution.py
@@ -8,9 +8,9 @@
 MESH = pl.DeviceIdType.MESH
 LOG2E = 1.4426950408889634
 SLOTS = 32
-READS = 8
+READS = 6
 BYROWS = 24
-STATS = 8
+STATS = 16
 SCORES = 4
 
 BLOCKS = (
@@ -41,7 +41,7 @@
 )
 LATE = (29, 30)
 FINAL = (31,)
-SPANS = ((0, 8), (8, 8), (16, 4), (20, 4), (24, 1), (25, 1), (26, 1), (27, 1), (28, 1))
+SPANS = ((0, 8), (8, 8), (16, 4), (20, 4), (24, 1), (25, 1), (26, 1), (27, 2))
 SUMS = {
     10: ("core0",),
     13: ("core1",),
@@ -51,10 +51,9 @@
     19: ("core4",),
     20: ("core5",),
     21: ("core6",),
-    22: ("core7",),
-    23: ("core8", "chip1"),
+    23: ("core7", "chip1"),
 }
-DRAIN = ("chip2", "chip3", "chip4", "chip5", "chip6", "late0", "chip7", "late1", "chip8", "final0")
+DRAIN = ("chip2", "chip3", "chip4", "chip5", "chip6", "late0", "late1", "chip7", "final0")
 
 def attend(q_hbm, k_hbm, v_hbm, o_ref, q_ref, buf, scores, weights, mine, theirs, own, part, from_core, pair, from_chip, late_pair, late_chip, late_core, final_in,
            q_sem, buf_sem, stats_out, stats_in, core_out, core_in, chip_out, chip_in, done_out, done_in, late_out, late_chip_in, late_core_in, final_sem):

time: 28.6 us -> 28.6 us (level)
  no operation moved by 1% of the time
where the time goes in v6:
time: 28.6 us; the launch traced here: 28.5 us
  Pallas kernels  27.7 us (97%)
  local copies, waits for them, and re-layouts  0.8 us (3%)
    pallas_call x1, Pallas kernels, step(): pl.pallas_call(attend, out_shape=jax.ShapeDtypeStruct(whole, jnp.bfloat16...  27.7 us
    unnamed x1, local copies, waits for them, and re-layouts  0.8 us

profile of v6, /device:TPU:0, one launch (start us, length us, event | category | flops | bytes accessed | tf_op | source)
XLA Modules:
  0.0 28.5 jit_solution(17476861647167634141)
XLA Ops:
  0.0 27.7 %attend.1 = bf16[32,32,256]{2,1,0:T(8,128)(2,1)S(1)} custom-call(bf16[32,32,256]{2,1,0:T(8,128)(2,1)} %q_hbm.1, bf16[32,2048,256]{2,1,0:T(8,128)(2,1)} %bitcast.2, bf16[32,2048,256]{2,1,0:T(8,128)(2,1)} %bitcast.3), custom_call_target="tpu_custom_call" | custom-call | tf_op jit(solution)/shard_map/attend/pallas_call | solution.py:240
  27.7 0.8 %copy.5 = bf16[32,32,256]{2,1,0:T(8,128)(2,1)} copy(bf16[32,32,256]{2,1,0:T(8,128)(2,1)S(1)} %attend.1) | data formatting | bytes 1048576

commit v7 on v6

--- a/solution.py
+++ b/solution.py
@@ -42,6 +42,7 @@
 LATE = (29, 30)
 FINAL = (31,)
 SPANS = ((0, 8), (8, 8), (16, 4), (20, 4), (24, 1), (25, 1), (26, 1), (27, 2))
+CHIP_SEM = (0, 1, 2, 2, 3, 3, 4, 5)
 SUMS = {
     10: ("core0",),
     13: ("core1",),
@@ -90,7 +91,7 @@
         return remote(part.at[span(c), other_rows], from_core.at[span(c)], core_out, core_in.at[c], core)
 
     def sums(c):
-        return remote(pair.at[span(c)], from_chip.at[span(c)], chip_out, chip_in.at[c], chip)
+        return remote(pair.at[span(c)], from_chip.at[span(c)], chip_out, chip_in.at[CHIP_SEM[c]], chip)
 
     def results(c):
         return remote(o_ref.at[span(c), rows], o_ref.at[span(c), rows], done_out, done_in, core)
@@ -99,7 +100,7 @@
         return remote(part.at[LATE[i]], late_chip.at[i], late_out, late_chip_in.at[i], chip)
 
     def to_core(i):
-        return remote(late_pair.at[i], late_core.at[i], late_out, late_core_in.at[i], core)
+        return remote(late_pair.at[i], late_core.at[i], late_out, late_core_in, core)
 
     def to_all(i, n):
         return remote(part.at[FINAL[i]], final_in.at[i, n], late_out, final_sem.at[i], peers[n])
@@ -159,7 +160,10 @@
             pair[span(i)] = add(own[span(i), rows], from_core[span(i)]).astype(jnp.bfloat16)
             sums(i).start()
         elif kind == "chip":
-            sums(i).wait_recv()
+            if i == 0 or CHIP_SEM[i] != CHIP_SEM[i - 1]:
+                joint = [SPANS[c] for c in range(len(SPANS)) if CHIP_SEM[c] == CHIP_SEM[i]]
+                arrived = from_chip.at[pl.ds(SPANS[i][0], sum(n for _, n in joint))]
+                remote(arrived, arrived, chip_out, chip_in.at[CHIP_SEM[i]], chip).wait_recv()
             o_ref[span(i), rows] = add(pair[span(i)], from_chip[span(i)]).astype(jnp.bfloat16)
             results(i).start()
         elif kind == "late":
@@ -217,8 +221,8 @@
 
     for what in DRAIN:
         sum_parts(what)
+    remote(late_core, late_core, late_out, late_core_in, core).wait_recv()
     for i, s in enumerate(LATE):
-        to_core(i).wait_recv()
         o_ref[s] = add(late_pair[i], late_core[i]).astype(jnp.bfloat16)
 
     summed = from_core.at[pl.ds(0, sum(n for _, n in SPANS))]
@@ -261,12 +265,12 @@
                 dma,
                 dma((len(SPANS),)),
                 dma,
-                dma((len(SPANS),)),
+                dma((max(CHIP_SEM) + 1,)),
                 dma,
                 dma,
                 dma,
                 dma((len(LATE),)),
-                dma((len(LATE),)),
+                dma,
                 dma((len(FINAL),)),
             ],
             compiler_params=pltpu.CompilerParams(collective_id=0, has_side_effects=True, vmem_limit_bytes=48 * 2**20),

time: 28.6 us -> 28.6 us (level)
  no operation moved by 1% of the time
where the time goes in v7:
time: 28.6 us; the launch traced here: 28.5 us
  Pallas kernels  27.7 us (97%)
  local copies, waits for them, and re-layouts  0.8 us (3%)
    pallas_call x1, Pallas kernels, step(): pl.pallas_call(attend, out_shape=jax.ShapeDtypeStruct(whole, jnp.bfloat16...  27.7 us
    unnamed x1, local copies, waits for them, and re-layouts  0.8 us

profile of v7, /device:TPU:0, one launch (start us, length us, event | category | flops | bytes accessed | tf_op | source)
XLA Modules:
  0.0 28.5 jit_solution(5238213933267935274)
XLA Ops:
  0.0 27.7 %attend.1 = bf16[32,32,256]{2,1,0:T(8,128)(2,1)S(1)} custom-call(bf16[32,32,256]{2,1,0:T(8,128)(2,1)} %q_hbm.1, bf16[32,2048,256]{2,1,0:T(8,128)(2,1)} %bitcast.2, bf16[32,2048,256]{2,1,0:T(8,128)(2,1)} %bitcast.3), custom_call_target="tpu_custom_call" | custom-call | tf_op jit(solution)/shard_map/attend/pallas_call | solution.py:244
  27.7 0.8 %copy.5 = bf16[32,32,256]{2,1,0:T(8,128)(2,1)} copy(bf16[32,32,256]{2,1,0:T(8,128)(2,1)S(1)} %attend.1) | data formatting | bytes 1048576
